TPU v7x, 32 devices: a whole 2x2x4 slice. The times are simulated.
32 devices in a mesh: replica: 2 (over core), model: 4 (over y, x), shift: 4 (over z).
Axes of the slice: x: 2, y: 2, z: 4, core: 2. Of those that a mesh axis runs over, the one named last changes fastest.
Arguments:
- partial_gate: float32 [8, 1024, 3072], P(('shift', 'replica'), None, 'model'), parts along dimension 0, may hold values from -0.875 to 0.875
- partial_up: float32 [8, 1024, 3072], P(('shift', 'replica'), None, 'model'), parts along dimension 0, may hold values from -0.875 to 0.875
- partial_down: float32 [8, 3072, 1024], P(('shift', 'replica'), 'model'), parts along dimension 0, may hold values from -0.875 to 0.875
- partial_norm: float32 [8, 1024], P(('shift', 'replica')), parts along dimension 0, may hold values from -8 to 8
- master_gate: float32 [4096, 3072], P(('shift', 'replica'), 'model'), parts along dimension 0, may hold values from -0.25 to 0.25
- master_up: float32 [4096, 3072], P(('shift', 'replica'), 'model'), parts along dimension 0, may hold values from -0.25 to 0.25
- master_down: float32 [12288, 1024], P(('shift', 'model'), 'replica'), parts along dimension 0, may hold values from -0.15625 to 0.15625
- master_norm: float32 [4096], P(('shift', 'replica')), parts along dimension 0, may hold values from 0.25 to 1.75
- memory_gate: float32 [4096, 3072], P(('shift', 'replica'), 'model'), parts along dimension 0, may hold values from -0.1875 to 0.1875
- memory_up: float32 [4096, 3072], P(('shift', 'replica'), 'model'), parts along dimension 0, may hold values from -0.1875 to 0.1875
- memory_down: float32 [12288, 1024], P(('shift', 'model'), 'replica'), parts along dimension 0, may hold values from -0.109375 to 0.109375
- memory_norm: float32 [4096], P(('shift', 'replica')), parts along dimension 0, may hold values from -1.75 to 1.75
Outputs:
- compute_gate: bfloat16 [4096, 3072], P('shift', 'model'), parts along dimension 0
- compute_up: bfloat16 [4096, 3072], P('shift', 'model'), parts along dimension 0
- compute_down: bfloat16 [12288, 1024], P(('shift', 'model')), parts along dimension 0
- compute_norm: bfloat16 [4096], P('shift'), parts along dimension 0
- stepped_gate: float32 [4096, 3072], P(('shift', 'replica'), 'model'), parts along dimension 0
- stepped_up: float32 [4096, 3072], P(('shift', 'replica'), 'model'), parts along dimension 0
- stepped_down: float32 [12288, 1024], P(('shift', 'model'), 'replica'), parts along dimension 0
- stepped_norm: float32 [4096], P(('shift', 'replica')), parts along dimension 0
- state_new_gate: float32 [4096, 3072], P(('shift', 'replica'), 'model'), parts along dimension 0
- state_new_up: float32 [4096, 3072], P(('shift', 'replica'), 'model'), parts along dimension 0
- state_new_down: float32 [12288, 1024], P(('shift', 'model'), 'replica'), parts along dimension 0
- state_new_norm: float32 [4096], P(('shift', 'replica')), parts along dimension 0
There are 4 independent parts, one for each index of `shift`. A program takes and returns all parts, laid end to end along the dimension named above; each array names one. Nothing has to cross between parts.
All inputs are finite; a program needn't handle non-finite values.
Results may differ from a plain program's by a relative error of at most 0.001.
Values may be sent and summed in bfloat16 or wider, within the bound.
A program may use at most 128 MiB of HBM per device.

v0:
```python
import functools
import math

import jax
import jax.numpy as jnp
from jax import lax
from jax.experimental import pallas as pl
from jax.experimental.pallas import tpu as pltpu
from jax.sharding import PartitionSpec as P

learn_rate = 0.5
hold_rate = 0.9
MESH = pl.DeviceIdType.MESH
LANES = 128


def cut(ref, axis, start, size):
    return ref.at[pl.ds(start, size), :] if axis == 0 else ref.at[:, pl.ds(start, size)]


def kernel(n, m, axes, *refs):
    refs = list(refs)
    take = lambda count: [refs.pop(0) for _ in range(count)]
    t = len(axes)
    partial, (partial_norm,) = take(t), take(1)
    master_hbm, (master_norm,) = take(t), take(1)
    memory_hbm, (memory_norm,) = take(t), take(1)
    compute, (compute_norm,) = take(t), take(1)
    stepped, (stepped_norm,) = take(t), take(1)
    state, (state_norm,) = take(t), take(1)
    got, memory = take(t), take(t)
    master, mean = stepped, state
    mean_n, got_n, master_n, memory_n, whole_n, line_n = take(6)
    own_line, own_got, slope_line, slope_got, fold, tile = take(6)
    load_sem, norm_load_sem = take(2)
    part_send, part_recv, comp_send, comp_recv = take(4)
    own_send, own_recv, slope_send, slope_recv = take(4)
    pn_send, pn_recv, wn_send, wn_recv = take(4)

    me = lax.axis_index("replica")
    at = lax.axis_index("model")
    rate = n ** (-0.5)
    peers = [lax.rem(me + k, n) for k in range(1, n)]
    mates = [lax.rem(at + k, m) for k in range(1, m)]

    chunks = []
    for which, axis in enumerate(axes):
        share = mean[which].shape[axis]
        chunks += [(which, c) for c in range(share // LANES)]
    count = len(chunks)

    def load(kind, number):
        which, c = chunks[number]
        axis = axes[which]
        share = mean[which].shape[axis]
        if kind == 0:
            source = cut(master_hbm[which], axis, c * LANES, LANES)
            target = master[which]
        elif kind == 1:
            start = pl.multiple_of(me * share + c * LANES, LANES)
            source = cut(partial[which].at[0], axis, start, LANES)
            target = mean[which]
        else:
            source = cut(memory_hbm[which], axis, c * LANES, LANES)
            target = memory[which]
        return pltpu.make_async_copy(
            source, cut(target, axis, c * LANES, LANES), load_sem.at[kind, number]
        )

    share_n = mean_n.shape[1]
    norm_loads = [
        pltpu.make_async_copy(
            partial_norm.at[:, pl.ds(pl.multiple_of(me * share_n, LANES), share_n)],
            mean_n,
            norm_load_sem.at[0],
        ),
        pltpu.make_async_copy(master_norm, master_n, norm_load_sem.at[1]),
        pltpu.make_async_copy(memory_norm, memory_n, norm_load_sem.at[2]),
    ]
    barrier = pltpu.get_barrier_semaphore()
    for peer in peers:
        pl.semaphore_signal(barrier, inc=1, device_id={"replica": peer}, device_id_type=MESH)
    for mate in mates:
        pl.semaphore_signal(barrier, inc=1, device_id={"model": mate}, device_id_type=MESH)
    for kind in range(3):
        for number in range(count):
            load(kind, number).start()
    for copy in norm_loads:
        copy.start()
    pl.semaphore_wait(barrier, n - 1 + m - 1)

    def part_copy(number, k):
        which, c = chunks[number]
        axis = axes[which]
        share = mean[which].shape[axis]
        start = pl.multiple_of(peers[k] * share + c * LANES, LANES)
        return pltpu.make_async_remote_copy(
            src_ref=cut(partial[which].at[0], axis, start, LANES),
            dst_ref=cut(got[which].at[k], axis, c * LANES, LANES),
            send_sem=part_send.at[number, k],
            recv_sem=part_recv.at[number, k],
            device_id={"replica": peers[k]},
            device_id_type=MESH,
        )

    def pn_copy(k):
        return pltpu.make_async_remote_copy(
            src_ref=partial_norm.at[
                :, pl.ds(pl.multiple_of(peers[k] * share_n, LANES), share_n)
            ],
            dst_ref=got_n.at[k],
            send_sem=pn_send.at[k],
            recv_sem=pn_recv.at[k],
            device_id={"replica": peers[k]},
            device_id_type=MESH,
        )

    for k in range(n - 1):
        pn_copy(k).start()
    for number in range(count):
        for k in range(n - 1):
            part_copy(number, k).start()

    def folded(square):
        return sum(
            square[:, j : j + LANES] for j in range(0, square.shape[1], LANES)
        )

    def line_of(number, block_of, rows, keep):
        which, c = chunks[number]
        if axes[which] == 0:
            height = 32
            for b in range(LANES // height):
                value = block_of(pl.ds(c * LANES + b * height, height), slice(None))
                if keep is not None:
                    keep[pl.ds(c * LANES + b * height, height), :] = value
                fold[pl.ds(b * height, height), :] = folded(value * value)
            return jnp.sum(fold[...].T, axis=0, keepdims=True)
        height = next(h for h in (128, 64, 32, 16, 8) if rows % h == 0)
        total = jnp.zeros((8, LANES), jnp.float32)
        lanes = pl.ds(c * LANES, LANES)
        for b in range(rows // height):
            value = block_of(pl.ds(b * height, height), lanes)
            if keep is not None:
                keep[pl.ds(b * height, height), lanes] = value
            total = total + jnp.sum((value * value).reshape(height // 8, 8, LANES), axis=0)
        return jnp.sum(total, axis=0, keepdims=True)

    def own_copy(k):
        return pltpu.make_async_remote_copy(
            src_ref=own_line,
            dst_ref=own_got.at[k],
            send_sem=own_send.at[k],
            recv_sem=own_recv.at[k],
            device_id={"model": mates[k]},
            device_id_type=MESH,
        )

    for number in range(count):
        which, c = chunks[number]
        load(0, number).wait()
        own_line[number] = line_of(
            number, lambda r, l: master[which][r, l], master[which].shape[0], None
        )
    for k in range(m - 1):
        own_copy(k).start()

    def wn_copy(k):
        mine = whole_n.at[:, pl.ds(pl.multiple_of(me * share_n, LANES), share_n)]
        return pltpu.make_async_remote_copy(
            src_ref=mine,
            dst_ref=mine,
            send_sem=wn_send.at[k],
            recv_sem=wn_recv.at[k],
            device_id={"replica": peers[k]},
            device_id_type=MESH,
        )

    for copy in norm_loads:
        copy.wait()
    total = mean_n[...]
    for k in range(n - 1):
        pn_copy(k).wait()
        total = total + got_n[k]
    new = hold_rate * memory_n[...] + total * rate
    state_norm[...] = new
    new = master_n[...] - learn_rate * new
    stepped_norm[...] = new
    whole_n[:, pl.ds(pl.multiple_of(me * share_n, LANES), share_n)] = new
    for k in range(n - 1):
        wn_copy(k).start()

    def slope_copy(number, k):
        return pltpu.make_async_remote_copy(
            src_ref=slope_line.at[number],
            dst_ref=slope_got.at[number, k],
            send_sem=slope_send.at[number, k],
            recv_sem=slope_recv.at[number, k],
            device_id={"model": mates[k]},
            device_id_type=MESH,
        )

    def reduce(number):
        which, c = chunks[number]
        load(1, number).wait()
        for k in range(n - 1):
            part_copy(number, k).wait_recv()

        def block(r, l):
            value = mean[which][r, l]
            for k in range(n - 1):
                value = value + got[which][k, r, l]
            return value * rate

        slope_line[number] = line_of(number, block, mean[which].shape[0], mean[which])
        for k in range(m - 1):
            slope_copy(number, k).start()

    def comp_copy(number, k):
        which, c = chunks[number]
        axis = axes[which]
        share = mean[which].shape[axis]
        mine = cut(compute[which], axis, pl.multiple_of(me * share + c * LANES, LANES), LANES)
        return pltpu.make_async_remote_copy(
            src_ref=mine,
            dst_ref=mine,
            send_sem=comp_send.at[number, k],
            recv_sem=comp_recv.at[number, k],
            device_id={"replica": peers[k]},
            device_id_type=MESH,
        )

    def update(number):
        which, c = chunks[number]
        axis = axes[which]
        share = mean[which].shape[axis]
        own, slope = own_line[number], slope_line[number]
        for k in range(m - 1):
            slope_copy(number, k).wait_recv()
            own = own + own_got[k, number]
            slope = slope + slope_got[number, k]
        ratio = jnp.sqrt(own) * lax.rsqrt(slope + 1e-06)
        load(2, number).wait()
        base = pl.multiple_of(me * share, LANES)

        def finish(r, l, r_out, l_out, scale):
            new = hold_rate * memory[which][r, l] + mean[which][r, l] * scale
            state[which][r, l] = new
            new = master[which][r, l] - learn_rate * new
            stepped[which][r, l] = new
            compute[which][r_out, l_out] = new.astype(jnp.bfloat16)

        if axis == 0:
            tile[...] = jnp.broadcast_to(ratio, (LANES, LANES)).T
            height, width = 32, mean[which].shape[1]
            for b in range(LANES // height):
                first = c * LANES + b * height
                finish(
                    pl.ds(first, height),
                    slice(None),
                    pl.ds(pl.multiple_of(base + first, height), height),
                    slice(None),
                    jnp.concatenate(
                        [tile[pl.ds(b * height, height), :]] * (width // LANES), axis=1
                    ),
                )
        else:
            rows = mean[which].shape[0]
            height = next(h for h in (128, 64, 32, 16, 8) if rows % h == 0)
            for b in range(rows // height):
                r = pl.ds(b * height, height)
                finish(
                    r,
                    pl.ds(c * LANES, LANES),
                    r,
                    pl.ds(pl.multiple_of(base + c * LANES, LANES), LANES),
                    ratio,
                )
        for k in range(n - 1):
            comp_copy(number, k).start()

    ahead = 8
    for number in range(count + ahead):
        if number < count:
            reduce(number)
        if number == ahead:
            for k in range(m - 1):
                own_copy(k).wait()
        if number >= ahead:
            update(number - ahead)

    for k in range(n - 1):
        wn_copy(k).wait()
    for j in range(whole_n.shape[1] // LANES):
        line_n[pl.ds(j, 1), :] = whole_n[:, j * LANES : (j + 1) * LANES]
    compute_norm[...] = line_n[...].astype(jnp.bfloat16)
    for number in range(count):
        for k in range(n - 1):
            part_copy(number, k).wait_send()
            comp_copy(number, k).wait()
        for k in range(m - 1):
            slope_copy(number, k).wait_send()


def drain(*refs):
    half = len(refs) // 2
    sems = refs[-1]
    copies = [
        pltpu.make_async_copy(refs[i], refs[half + i], sems.at[i]) for i in range(half)
    ]
    for copy in copies:
        copy.start()
    for copy in copies:
        copy.wait()


def exchange(n, m, args):
    axes = (0, 0, 1)
    partial, partial_norm = args[0:3], args[3]
    master, master_norm = args[4:7], args[7]
    memory, memory_norm = args[8:11], args[11]
    row = lambda x: x.reshape(1, -1)
    shapes = [x.shape for x in master]
    count = sum(s[a] // LANES for s, a in zip(shapes, axes))
    share_n, width_n = master_norm.shape[0], partial_norm.shape[1]
    f32, bf16 = jnp.float32, jnp.bfloat16
    dma = lambda *s: pltpu.SemaphoreType.DMA(s)
    out_shape = (
        [pltpu.VMEM(x.shape[1:], bf16) for x in partial]
        + [pltpu.VMEM((width_n // LANES, LANES), bf16)]
        + ([pltpu.VMEM(s, f32) for s in shapes] + [pltpu.VMEM((1, share_n), f32)]) * 2
    )
    scratch = (
        [pltpu.VMEM((n - 1,) + s, f32) for s in shapes]
        + [pltpu.VMEM(s, f32) for s in shapes]
        + [
            pltpu.VMEM((1, share_n), f32),
            pltpu.VMEM((n - 1, 1, share_n), f32),
            pltpu.VMEM((1, share_n), f32),
            pltpu.VMEM((1, share_n), f32),
            pltpu.VMEM((1, width_n), f32),
            pltpu.VMEM((width_n // LANES, LANES), f32),
            pltpu.VMEM((count, 1, LANES), f32),
            pltpu.VMEM((m - 1, count, 1, LANES), f32),
            pltpu.VMEM((count, 1, LANES), f32),
            pltpu.VMEM((count, m - 1, 1, LANES), f32),
            pltpu.VMEM((LANES, LANES), f32),
            pltpu.VMEM((LANES, LANES), f32),
            dma(3, count),
            dma(3),
        ]
        + [dma(count, n - 1)] * 4
        + [dma(m - 1)] * 2
        + [dma(count, m - 1)] * 2
        + [dma(n - 1)] * 4
    )
    results = sum(math.prod(x.shape) * jnp.dtype(x.dtype).itemsize for x in out_shape)
    room = 63 * 2**20 - results
    outs = pl.pallas_call(
        functools.partial(kernel, n, m, axes),
        out_shape=out_shape,
        in_specs=[pl.BlockSpec(memory_space=pltpu.HBM)] * 12,
        out_specs=[pl.BlockSpec(memory_space=pltpu.VMEM)] * 12,
        scratch_shapes=scratch,
        compiler_params=pltpu.CompilerParams(
            collective_id=0, has_side_effects=True, vmem_limit_bytes=room
        ),
    )(
        *partial, partial_norm, *master, row(master_norm), *memory, row(memory_norm)
    )
    outs = pl.pallas_call(
        drain,
        out_shape=[jax.ShapeDtypeStruct(x.shape, x.dtype) for x in outs],
        in_specs=[pl.BlockSpec(memory_space=pl.ANY)] * len(outs),
        out_specs=[pl.BlockSpec(memory_space=pltpu.HBM)] * len(outs),
        scratch_shapes=[dma(len(outs))],
        compiler_params=pltpu.CompilerParams(vmem_limit_bytes=2**20),
    )(*outs)
    return [x.reshape(-1) if i % 4 == 3 else x for i, x in enumerate(outs)]


def plain(args):
    partial, master, memory = args[0:4], args[4:8], args[8:12]
    n = lax.axis_size("replica")
    axes = (0, 0, 1, 0)
    mean = [
        lax.psum_scatter(p[0], "replica", scatter_dimension=a, tiled=True) * n ** (-0.5)
        for p, a in zip(partial, axes)
    ]
    square = lambda x, a: jnp.sum(x * x, axis=1 - a, keepdims=True)
    own, slope = lax.psum(
        (
            [square(x, a) for x, a in zip(master[:3], axes)],
            [square(x, a) for x, a in zip(mean[:3], axes)],
        ),
        "model",
    )
    mean = [
        x * (jnp.sqrt(o) * lax.rsqrt(s + 1e-06)) for x, o, s in zip(mean[:3], own, slope)
    ] + mean[3:]
    state = [hold_rate * e + x for e, x in zip(memory, mean)]
    stepped = [w - learn_rate * s for w, s in zip(master, state)]
    compute = [
        lax.all_gather(s.astype(jnp.bfloat16), "replica", axis=a, tiled=True)
        for s, a in zip(stepped, axes)
    ]
    return compute + stepped + state


def on_device(*args):
    n, m = lax.axis_size("replica"), lax.axis_size("model")
    shares = (args[4].shape[0], args[5].shape[0], args[6].shape[1], args[7].shape[0])
    if n > 1 and m > 1 and all(s % LANES == 0 for s in shares):
        return tuple(exchange(n, m, args))
    return tuple(plain(args))


def solution(mesh):
    partial = P(("shift", "replica"), None, "model")
    rows, columns = P(("shift", "replica"), "model"), P(("shift", "model"), "replica")
    vector = P(("shift", "replica"))
    own = (rows, rows, columns, vector)
    return jax.shard_map(
        on_device,
        mesh=mesh,
        in_specs=(
            partial,
            partial,
            P(("shift", "replica"), "model", None),
            P(("shift", "replica"), None),
        )
        + own
        + own,
        out_specs=(
            P("shift", "model"),
            P("shift", "model"),
            P(("shift", "model"), None),
            P("shift"),
        )
        + own
        + own,
        check_vma=False,
    )
```

profile of v0, /device:TPU:0, one launch (start us, length us, event | category | flops | bytes accessed | tf_op | source)
XLA Modules:
  0.0 22.9 jit_solution(2356192947406264631)
XLA Ops:
  0.6 17.1 %shard_map.211 = (bf16[1024,768]{1,0:T(8,128)(2,1)S(1)}, bf16[1024,768]{1,0:T(8,128)(2,1)S(1)}, bf16[768,1024]{1,0:T(8,128)(2,1)S(1)}, bf16[8,128]{1,0:T(8,128)(...) custom-call(f32[1,1024,768]{2,1,0:T(8,128)} %refs_0_.1, ...), custom_call_target="tpu_custom_call" | custom-call | tf_op jit(solution)/shard_map/pallas_call | solution.py:359
  17.7 5.2 %shard_map.212 = (bf16[1024,768]{1,0:T(8,128)(2,1)}, bf16[1024,768]{1,0:T(8,128)(2,1)}, bf16[768,1024]{1,0:T(8,128)(2,1)}, bf16[8,128]{1,0:T(8,128)(2,1)}, f32[5...) custom-call(bf16[1024,768]{1,0:T(8,128)(2,1)S(1)} %get-tuple-element, ...), custom_call_target="tpu_custom_call" | custom-call | tf_op jit(solution)/shard_map/pallas_call | solution.py:371
where the time goes:
time: 23.1 us; the launch traced here: 22.9 us
  Pallas kernels  22.3 us (97%)
  between operations  0.66 us (3%)
    pallas_call x1, Pallas kernels, exchange(): pl.pallas_call(functools.partial(kernel, n, m, axes), out_shape=out_shape...  17.1 us
    pallas_call x1, Pallas kernels, exchange(): pl.pallas_call(drain, out_shape=[jax.ShapeDtypeStruct(x.shape, x.dtype) f...  5.19 us

commit v1 on v0

v1 whole, which is shorter than its diff:
```python
import functools
import math

import jax
import jax.numpy as jnp
from jax import lax
from jax.experimental import pallas as pl
from jax.experimental.pallas import tpu as pltpu
from jax.sharding import PartitionSpec as P

learn_rate = 0.5
hold_rate = 0.9
MESH = pl.DeviceIdType.MESH
LANES = 128
CODE_SCALE = 2.0**13


def cut(ref, axis, start, size):
    return ref.at[pl.ds(start, size), :] if axis == 0 else ref.at[:, pl.ds(start, size)]


def code(x):
    x = x * CODE_SCALE
    x = x * x * x
    return (x * x * x).astype(jnp.bfloat16)


def decode(y):
    y = y.astype(jnp.float32)
    size = jnp.maximum(jnp.abs(y), 2.0**-126)
    return y * lax.exp2(lax.log2(size) * (-8 / 9) - math.log2(CODE_SCALE))


def kernel(m, axes, *refs):
    refs = list(refs)
    take = lambda count: [refs.pop(0) for _ in range(count)]
    t = len(axes)
    partial, (partial_norm,) = take(t), take(1)
    master_hbm, (master_norm,) = take(t), take(1)
    memory_hbm, (memory_norm,) = take(t), take(1)
    compute, (compute_norm,) = take(t), take(1)
    stepped, (stepped_norm,) = take(t), take(1)
    state, (state_norm,) = take(t), take(1)
    other, sent, got, memory = take(t), take(t), take(t), take(t)
    master, mean = stepped, state
    mean_n, got_n, master_n, memory_n, whole_n, line_n = take(6)
    line, line_got, fold, tile = take(4)
    load_sem, part_send, part_recv, comp_send, comp_recv = take(5)
    line_send, line_recv, norm_load_sem, norm_send, norm_recv, ready = take(6)

    me = lax.axis_index("replica")
    at = lax.axis_index("model")
    peer = 1 - me
    rate = 2 ** (-0.5)
    mates = [lax.rem(at + k, m) for k in range(1, m)]

    chunks = []
    for which, axis in enumerate(axes):
        share = mean[which].shape[axis]
        chunks += [(which, c) for c in range(share // LANES)]
    chunks.insert(0, chunks.pop(chunks.index((t - 1, 0))))
    count, lead = len(chunks), 4

    def load(kind, number):
        which, c = chunks[number]
        axis = axes[which]
        share = mean[which].shape[axis]
        source = (partial[which].at[0], partial[which].at[0], master_hbm[which], memory_hbm[which])
        target = (other, mean, master, memory)[kind][which]
        start = ((peer, me)[kind] * share if kind < 2 else 0) + c * LANES
        start = pl.multiple_of(start, LANES)
        return pltpu.make_async_copy(
            cut(source[kind], axis, start, LANES),
            cut(target, axis, c * LANES, LANES),
            load_sem.at[(number - lead) % (count + lead) if kind == 0 else number],
        )

    def wait_loads(number):
        size = (3 if number + lead < count else 2) * LANES
        pltpu.make_async_copy(
            master_hbm[0].at[pl.ds(0, size), :],
            master[0].at[pl.ds(0, size), :],
            load_sem.at[number],
        ).wait()

    share_n = mean_n.shape[1]
    own_n = pl.ds(pl.multiple_of(me * share_n, LANES), share_n)
    norm_loads = [
        pltpu.make_async_copy(partial_norm.at[:, own_n], mean_n, norm_load_sem.at[0]),
        pltpu.make_async_copy(master_norm, master_n, norm_load_sem.at[1]),
        pltpu.make_async_copy(memory_norm, memory_n, norm_load_sem.at[2]),
    ]

    def to_peer(source, target, send, recv):
        return pltpu.make_async_remote_copy(
            src_ref=source,
            dst_ref=target,
            send_sem=send,
            recv_sem=recv,
            device_id={"replica": peer},
            device_id_type=MESH,
        )

    def part_copy(number):
        which, c = chunks[number]
        return to_peer(
            sent[which].at[c], got[which].at[c], part_send.at[which], part_recv.at[number]
        )

    def comp_copy(number):
        which, c = chunks[number]
        axis = axes[which]
        share = mean[which].shape[axis]
        mine = cut(compute[which], axis, pl.multiple_of(me * share + c * LANES, LANES), LANES)
        return to_peer(mine, mine, comp_send.at[which], comp_recv.at[which])

    def comp_half(which):
        axis = axes[which]
        share = mean[which].shape[axis]
        mine = cut(compute[which], axis, pl.multiple_of(me * share, LANES), share)
        return to_peer(mine, mine, comp_send.at[which], comp_recv.at[which])

    peer_n = pl.ds(pl.multiple_of(peer * share_n, LANES), share_n)
    part_norm_copy = to_peer(partial_norm.at[:, peer_n], got_n, norm_send.at[0], norm_recv.at[0])
    whole_norm_copy = to_peer(
        whole_n.at[:, own_n], whole_n.at[:, own_n], norm_send.at[1], norm_recv.at[1]
    )

    def to_mate(source, target, recv, k):
        return pltpu.make_async_remote_copy(
            src_ref=source,
            dst_ref=target,
            send_sem=line_send.at[0],
            recv_sem=recv,
            device_id={"model": mates[k]},
            device_id_type=MESH,
        )

    def line_copy(number, k):
        return to_mate(line.at[number], line_got.at[number, k], line_recv.at[number], k)

    def blocks(number):
        which, c = chunks[number]
        rows, columns = mean[which].shape
        if axes[which] == 0:
            height = 32
            for b in range(LANES // height):
                inside = (pl.ds(b * height, height), slice(None))
                yield inside, (pl.ds(c * LANES + b * height, height), slice(None))
        else:
            height = next(h for h in (128, 64, 32, 16, 8) if rows % h == 0)
            for b in range(rows // height):
                r = pl.ds(b * height, height)
                yield (r, slice(None)), (r, pl.ds(c * LANES, LANES))

    def prepare(number):
        which, c = chunks[number]
        for inside, block in blocks(number):
            sent[which][(c, *inside)] = code(other[which][block])

    def squares(number, row, block_of):
        which, c = chunks[number]
        if axes[which] == 0:
            for inside, block in blocks(number):
                value = block_of(inside, block)
                value = value * value
                fold[number % 2, row, inside[0], :] = sum(
                    value[:, j : j + LANES] for j in range(0, value.shape[1], LANES)
                )
        else:
            total = jnp.zeros((8, LANES), jnp.float32)
            for inside, block in blocks(number):
                value = block_of(inside, block)
                total = total + jnp.sum((value * value).reshape(-1, 8, LANES), axis=0)
            line[number, row : row + 1, :] = jnp.sum(total, axis=0, keepdims=True)

    def reduce(number):
        which, c = chunks[number]

        def total(inside, block):
            value = mean[which][block] + decode(got[which][(c, *inside)])
            mean[which][block] = value
            return value

        squares(number, 0, lambda inside, block: master[which][block])
        squares(number, 1, total)

    def turn(number):
        if axes[chunks[number][0]] == 0:
            for row in range(2):
                line[number, row : row + 1, :] = jnp.sum(
                    fold[number % 2, row].T, axis=0, keepdims=True
                )

    def send_line(number):
        for k in range(m - 1):
            line_copy(number, k).start()

    def ratio_of(number):
        both = line[number]
        for k in range(m - 1):
            both = both + line_got[number, k]
        own, slope = both[0:1], both[1:2]
        return jnp.sqrt(own) * lax.rsqrt(slope * rate**2 + 1e-06) * rate

    def wait_line(number):
        to_mate(line_got.at[number], line_got.at[number], line_recv.at[number], 0).wait_recv()

    def spread(number):
        tile[number % 2] = jnp.broadcast_to(ratio_of(number), (LANES, LANES)).T

    def update(number):
        which, c = chunks[number]
        axis = axes[which]
        share = mean[which].shape[axis]
        base = pl.multiple_of(me * share + c * LANES, LANES)
        if axis == 1:
            ratio = ratio_of(number)
        for inside, block in blocks(number):
            if axis == 0:
                scale = jnp.concatenate(
                    [tile[number % 2, inside[0], :]] * (mean[which].shape[1] // LANES), axis=1
                )
                first = inside[0].start
                target = (pl.ds(pl.multiple_of(base + first, 32), inside[0].size), slice(None))
            else:
                scale = ratio
                target = (inside[0], pl.ds(base, LANES))
            new = hold_rate * memory[which][block] + mean[which][block] * scale
            state[which][block] = new
            new = master[which][block] - learn_rate * new
            stepped[which][block] = new
            compute[which][target] = new.astype(jnp.bfloat16)

    def norm():
        for copy in norm_loads:
            copy.wait()
        part_norm_copy.wait()
        new = hold_rate * memory_n[...] + (mean_n[...] + got_n[...]) * rate
        state_norm[...] = new
        new = master_n[...] - learn_rate * new
        stepped_norm[...] = new
        whole_n[:, own_n] = new
        whole_norm_copy.start()

    barrier = pltpu.get_barrier_semaphore()

    def signal(target, **where):
        pl.semaphore_signal(target, inc=1, device_id=where, device_id_type=MESH)

    @pl.when(me == 0)
    def _():
        signal(barrier, replica=peer)
        for mate in mates:
            signal(barrier, model=mate)

    @pl.when(me == 1)
    def _():
        for mate in mates:
            signal(barrier, model=mate, replica=peer)

    for number in range(count + lead):
        if number < count:
            load(0, number).start()
        if number == lead:
            for copy in norm_loads:
                copy.start()
        if number + 1 >= lead and number + 1 - lead < count:
            load(2, number + 1 - lead).start()
            load(1, number + 1 - lead).start()

    @pl.when(me == 1)
    def _():
        pl.semaphore_wait(barrier, 1)
        signal(ready, replica=peer)

    @pl.when(me == 0)
    def _():
        pl.semaphore_wait(ready, 1)

    for number in range(lead):
        load(0, number).wait()
        prepare(number)
        part_copy(number).start()
    part_norm_copy.start()
    for number in range(count):
        wait_loads(number)
        part_copy(number).wait_recv()
        if number > 0:
            turn(number - 1)
        reduce(number)
        if number + lead < count:
            prepare(number + lead)
            part_copy(number + lead).start()
        load(3, number).start()
        if number == 0:

            @pl.when(me == 0)
            def _():
                pl.semaphore_wait(barrier, 2 * (m - 1))
                signal(ready, replica=peer)

            @pl.when(me == 1)
            def _():
                pl.semaphore_wait(ready, 1)

        if number > 0 and axes[chunks[number - 1][0]] == 0:
            send_line(number - 1)
        if axes[chunks[number][0]] == 1:
            send_line(number)
    if axes[chunks[-1][0]] == 0:
        turn(count - 1)
        send_line(count - 1)
    norm()

    for number in range(count):
        load(3, number).wait()
        wait_line(number)
        if axes[chunks[number][0]] == 0:
            spread(number)
        update(number)
        comp_copy(number).start()

    whole_norm_copy.wait()
    for j in range(whole_n.shape[1] // LANES):
        line_n[pl.ds(j, 1), :] = whole_n[:, j * LANES : (j + 1) * LANES]
    compute_norm[...] = line_n[...].astype(jnp.bfloat16)
    for which in range(t):
        to_peer(sent[which], got[which], part_send.at[which], part_recv.at[0]).wait_send()
        comp_half(which).wait()
    to_mate(line_got, line_got, line_recv.at[0], 0).wait_send()


def drain(*refs):
    half = len(refs) // 2
    sems = refs[-1]
    copies = [
        pltpu.make_async_copy(refs[i], refs[half + i], sems.at[i]) for i in range(half)
    ]
    for copy in copies:
        copy.start()
    for copy in copies:
        copy.wait()


def exchange(m, args):
    axes = (0, 0, 1)
    partial, partial_norm = args[0:3], args[3]
    master, master_norm = args[4:7], args[7]
    memory, memory_norm = args[8:11], args[11]
    row = lambda x: x.reshape(1, -1)
    shapes = [x.shape for x in master]
    counts = [s[a] // LANES for s, a in zip(shapes, axes)]
    pieces = [
        (c, LANES, s[1]) if a == 0 else (c, s[0], LANES)
        for s, a, c in zip(shapes, axes, counts)
    ]
    count = sum(counts)
    share_n, width_n = master_norm.shape[0], partial_norm.shape[1]
    f32, bf16 = jnp.float32, jnp.bfloat16
    dma = lambda *s: pltpu.SemaphoreType.DMA(s)
    out_shape = (
        [pltpu.VMEM(x.shape[1:], bf16) for x in partial]
        + [pltpu.VMEM((width_n // LANES, LANES), bf16)]
        + ([pltpu.VMEM(s, f32) for s in shapes] + [pltpu.VMEM((1, share_n), f32)]) * 2
    )
    scratch = (
        [pltpu.VMEM(s, f32) for s in shapes]
        + [pltpu.VMEM(s, bf16) for s in pieces] * 2
        + [pltpu.VMEM(s, f32) for s in shapes]
        + [pltpu.VMEM((1, share_n), f32)] * 4
        + [
            pltpu.VMEM((1, width_n), f32),
            pltpu.VMEM((width_n // LANES, LANES), f32),
            pltpu.VMEM((count, 2, LANES), f32),
            pltpu.VMEM((count, m - 1, 2, LANES), f32),
            pltpu.VMEM((2, 2, LANES, LANES), f32),
            pltpu.VMEM((2, LANES, LANES), f32),
            dma(count + 4),
            dma(len(shapes)),
            dma(count),
            dma(len(shapes)),
            dma(len(shapes)),
            dma(1),
            dma(count),
            dma(3),
            dma(2),
            dma(2),
            pltpu.SemaphoreType.REGULAR,
        ]
    )
    results = sum(math.prod(x.shape) * jnp.dtype(x.dtype).itemsize for x in out_shape)
    room = 63 * 2**20 - results
    outs = pl.pallas_call(
        functools.partial(kernel, m, axes),
        out_shape=out_shape,
        in_specs=[pl.BlockSpec(memory_space=pltpu.HBM)] * 12,
        out_specs=[pl.BlockSpec(memory_space=pltpu.VMEM)] * 12,
        scratch_shapes=scratch,
        compiler_params=pltpu.CompilerParams(
            collective_id=0, has_side_effects=True, vmem_limit_bytes=room
        ),
    )(
        *partial, partial_norm, *master, row(master_norm), *memory, row(memory_norm)
    )
    outs = pl.pallas_call(
        drain,
        out_shape=[jax.ShapeDtypeStruct(x.shape, x.dtype) for x in outs],
        in_specs=[pl.BlockSpec(memory_space=pl.ANY)] * len(outs),
        out_specs=[pl.BlockSpec(memory_space=pltpu.HBM)] * len(outs),
        scratch_shapes=[dma(len(outs))],
        compiler_params=pltpu.CompilerParams(vmem_limit_bytes=2**20),
    )(*outs)
    return [x.reshape(-1) if i % 4 == 3 else x for i, x in enumerate(outs)]


def plain(args):
    partial, master, memory = args[0:4], args[4:8], args[8:12]
    n = lax.axis_size("replica")
    axes = (0, 0, 1, 0)
    mean = [
        lax.psum_scatter(p[0], "replica", scatter_dimension=a, tiled=True) * n ** (-0.5)
        for p, a in zip(partial, axes)
    ]
    square = lambda x, a: jnp.sum(x * x, axis=1 - a, keepdims=True)
    own, slope = lax.psum(
        (
            [square(x, a) for x, a in zip(master[:3], axes)],
            [square(x, a) for x, a in zip(mean[:3], axes)],
        ),
        "model",
    )
    mean = [
        x * (jnp.sqrt(o) * lax.rsqrt(s + 1e-06)) for x, o, s in zip(mean[:3], own, slope)
    ] + mean[3:]
    state = [hold_rate * e + x for e, x in zip(memory, mean)]
    stepped = [w - learn_rate * s for w, s in zip(master, state)]
    compute = [
        lax.all_gather(s.astype(jnp.bfloat16), "replica", axis=a, tiled=True)
        for s, a in zip(stepped, axes)
    ]
    return compute + stepped + state


def on_device(*args):
    n, m = lax.axis_size("replica"), lax.axis_size("model")
    gate, up, down, gain = (x.shape for x in args[4:8])
    shares = (gate[0], up[0], down[1], gain[0])
    if (
        n == 2
        and m > 1
        and all(s % LANES == 0 and s >= 3 * LANES for s in shares)
        and gate[1] == up[1] == down[0]
    ):
        return tuple(exchange(m, args))
    return tuple(plain(args))


def solution(mesh):
    partial = P(("shift", "replica"), None, "model")
    rows, columns = P(("shift", "replica"), "model"), P(("shift", "model"), "replica")
    vector = P(("shift", "replica"))
    own = (rows, rows, columns, vector)
    return jax.shard_map(
        on_device,
        mesh=mesh,
        in_specs=(
            partial,
            partial,
            P(("shift", "replica"), "model", None),
            P(("shift", "replica"), None),
        )
        + own
        + own,
        out_specs=(
            P("shift", "model"),
            P("shift", "model"),
            P(("shift", "model"), None),
            P("shift"),
        )
        + own
        + own,
        check_vma=False,
    )
```

time: 23.1 us -> 19.6 us (0.85)
  Pallas kernels: 22.3 us -> 18.8 us
    pallas_call x1, Pallas kernels: 17.1 us -> 13.6 us  [exchange(): pl.pallas_call(functools.partial(kernel, m, axes), out_shape=out_shape, i...]
where the time goes in v1:
time: 19.6 us; the launch traced here: 19.4 us
  Pallas kernels  18.8 us (96%)
  between operations  0.66 us (3%)
    pallas_call x1, Pallas kernels, exchange(): pl.pallas_call(functools.partial(kernel, m, axes), out_shape=out_shape, i...  13.6 us
    pallas_call x1, Pallas kernels, exchange(): pl.pallas_call(drain, out_shape=[jax.ShapeDtypeStruct(x.shape, x.dtype) f...  5.19 us

profile of v1, /device:TPU:0, one launch (start us, length us, event | category | flops | bytes accessed | tf_op | source)
XLA Modules:
  0.0 19.4 jit_solution(8680542235776257971)
XLA Ops:
  0.6 13.6 %shard_map.211 = (bf16[1024,768]{1,0:T(8,128)(2,1)S(1)}, bf16[1024,768]{1,0:T(8,128)(2,1)S(1)}, bf16[768,1024]{1,0:T(8,128)(2,1)S(1)}, bf16[8,128]{1,0:T(8,128)(...) custom-call(f32[1,1024,768]{2,1,0:T(8,128)} %refs_0_.1, ...), custom_call_target="tpu_custom_call" | custom-call | tf_op jit(solution)/shard_map/pallas_call | solution.py:394
  14.2 5.2 %shard_map.212 = (bf16[1024,768]{1,0:T(8,128)(2,1)}, bf16[1024,768]{1,0:T(8,128)(2,1)}, bf16[768,1024]{1,0:T(8,128)(2,1)}, bf16[8,128]{1,0:T(8,128)(2,1)}, f32[5...) custom-call(bf16[1024,768]{1,0:T(8,128)(2,1)S(1)} %get-tuple-element, ...), custom_call_target="tpu_custom_call" | custom-call | tf_op jit(solution)/shard_map/pallas_call | solution.py:406

commit v2 on v1

--- a/solution.py
+++ b/solution.py
@@ -31,7 +31,25 @@
     return y * lax.exp2(lax.log2(size) * (-8 / 9) - math.log2(CODE_SCALE))
 
 
-def kernel(m, axes, *refs):
+def kernel(m, axes, count, *refs):
+    sems = lambda *shape: pltpu.SemaphoreType.DMA(shape)
+    pl.run_scoped(
+        functools.partial(body, m, axes, refs),
+        sems(count + 8),
+        sems(len(axes)),
+        sems(count),
+        sems(len(axes)),
+        sems(1),
+        sems(count),
+        sems(1),
+        sems(2),
+        sems(2),
+        pltpu.SemaphoreType.REGULAR,
+    )
+
+
+def body(m, axes, refs, load_sem, part_send, part_recv, comp_recv, *more):
+    line_send, line_recv, norm_load_sem, norm_send, norm_recv, ready = more
     refs = list(refs)
     take = lambda count: [refs.pop(0) for _ in range(count)]
     t = len(axes)
@@ -43,10 +61,8 @@
     state, (state_norm,) = take(t), take(1)
     other, sent, got, memory = take(t), take(t), take(t), take(t)
     master, mean = stepped, state
-    mean_n, got_n, master_n, memory_n, whole_n, line_n = take(6)
+    own_norm, got_n, whole_n, line_n = take(4)
     line, line_got, fold, tile = take(4)
-    load_sem, part_send, part_recv, comp_send, comp_recv = take(5)
-    line_send, line_recv, norm_load_sem, norm_send, norm_recv, ready = take(6)
 
     me = lax.axis_index("replica")
     at = lax.axis_index("model")
@@ -58,8 +74,14 @@
     for which, axis in enumerate(axes):
         share = mean[which].shape[axis]
         chunks += [(which, c) for c in range(share // LANES)]
-    chunks.insert(0, chunks.pop(chunks.index((t - 1, 0))))
-    count, lead = len(chunks), 4
+    for c in range(2):
+        chunks.insert(c, chunks.pop(chunks.index((t - 1, c))))
+    count, lead = len(chunks), 8
+
+    def slot_of(kind, number):
+        if kind == 0:
+            return count + number if number < lead else number + 1 - lead
+        return number
 
     def load(kind, number):
         which, c = chunks[number]
@@ -72,23 +94,22 @@
         return pltpu.make_async_copy(
             cut(source[kind], axis, start, LANES),
             cut(target, axis, c * LANES, LANES),
-            load_sem.at[(number - lead) % (count + lead) if kind == 0 else number],
+            load_sem.at[slot_of(kind, number)],
         )
 
     def wait_loads(number):
-        size = (3 if number + lead < count else 2) * LANES
+        size = (3 if 0 < number <= count - lead else 2) * LANES
         pltpu.make_async_copy(
             master_hbm[0].at[pl.ds(0, size), :],
             master[0].at[pl.ds(0, size), :],
             load_sem.at[number],
         ).wait()
 
-    share_n = mean_n.shape[1]
+    share_n = got_n.shape[1]
     own_n = pl.ds(pl.multiple_of(me * share_n, LANES), share_n)
     norm_loads = [
-        pltpu.make_async_copy(partial_norm.at[:, own_n], mean_n, norm_load_sem.at[0]),
-        pltpu.make_async_copy(master_norm, master_n, norm_load_sem.at[1]),
-        pltpu.make_async_copy(memory_norm, memory_n, norm_load_sem.at[2]),
+        pltpu.make_async_copy(source, own_norm.at[i], norm_load_sem.at[0])
+        for i, source in enumerate((partial_norm.at[:, own_n], master_norm, memory_norm))
     ]
 
     def to_peer(source, target, send, recv):
@@ -112,13 +133,13 @@
         axis = axes[which]
         share = mean[which].shape[axis]
         mine = cut(compute[which], axis, pl.multiple_of(me * share + c * LANES, LANES), LANES)
-        return to_peer(mine, mine, comp_send.at[which], comp_recv.at[which])
+        return to_peer(mine, mine, part_send.at[which], comp_recv.at[which])
 
     def comp_half(which):
         axis = axes[which]
         share = mean[which].shape[axis]
         mine = cut(compute[which], axis, pl.multiple_of(me * share, LANES), share)
-        return to_peer(mine, mine, comp_send.at[which], comp_recv.at[which])
+        return to_peer(mine, mine, part_send.at[which], comp_recv.at[which])
 
     peer_n = pl.ds(pl.multiple_of(peer * share_n, LANES), share_n)
     part_norm_copy = to_peer(partial_norm.at[:, peer_n], got_n, norm_send.at[0], norm_recv.at[0])
@@ -233,12 +254,11 @@
             compute[which][target] = new.astype(jnp.bfloat16)
 
     def norm():
-        for copy in norm_loads:
-            copy.wait()
+        pltpu.make_async_copy(own_norm, own_norm, norm_load_sem.at[0]).wait()
         part_norm_copy.wait()
-        new = hold_rate * memory_n[...] + (mean_n[...] + got_n[...]) * rate
+        new = hold_rate * own_norm[2] + (own_norm[0] + got_n[...]) * rate
         state_norm[...] = new
-        new = master_n[...] - learn_rate * new
+        new = own_norm[1] - learn_rate * new
         stepped_norm[...] = new
         whole_n[:, own_n] = new
         whole_norm_copy.start()
@@ -247,6 +267,12 @@
 
     def signal(target, **where):
         pl.semaphore_signal(target, inc=1, device_id=where, device_id_type=MESH)
+
+    for number in range(lead):
+        load(0, number).start()
+        if number == 2:
+            load(2, 0).start()
+            load(1, 0).start()
 
     @pl.when(me == 0)
     def _():
@@ -259,15 +285,15 @@
         for mate in mates:
             signal(barrier, model=mate, replica=peer)
 
-    for number in range(count + lead):
-        if number < count:
-            load(0, number).start()
-        if number == lead:
+    for number in range(count):
+        if 0 < number <= count - lead:
+            load(0, number + lead - 1).start()
+        if number > 0:
+            load(2, number).start()
+            load(1, number).start()
+        if number == 0:
             for copy in norm_loads:
                 copy.start()
-        if number + 1 >= lead and number + 1 - lead < count:
-            load(2, number + 1 - lead).start()
-            load(1, number + 1 - lead).start()
 
     @pl.when(me == 1)
     def _():
@@ -283,16 +309,28 @@
         prepare(number)
         part_copy(number).start()
     part_norm_copy.start()
+    turned = 0
     for number in range(count):
         wait_loads(number)
         part_copy(number).wait_recv()
-        if number > 0:
+        ready_lines = [number] if axes[chunks[number][0]] == 1 else []
+        if turned < number:
             turn(number - 1)
+            ready_lines.insert(0, number - 1)
+            turned = number
         reduce(number)
-        if number + lead < count:
-            prepare(number + lead)
-            part_copy(number + lead).start()
-        load(3, number).start()
+        if axes[chunks[number][0]] == 1:
+            turned = number + 1
+        if 0 < number <= count - lead:
+            if turned == number:
+                turn(number)
+                ready_lines.append(number)
+                turned = number + 1
+            prepare(number + lead - 1)
+            part_copy(number + lead - 1).start()
+        for later in range(2 * (number - 6), 2 * (number - 5)):
+            if 0 <= later < count:
+                load(3, later).start()
         if number == 0:
 
             @pl.when(me == 0)
@@ -304,14 +342,14 @@
             def _():
                 pl.semaphore_wait(ready, 1)
 
-        if number > 0 and axes[chunks[number - 1][0]] == 0:
-            send_line(number - 1)
-        if axes[chunks[number][0]] == 1:
-            send_line(number)
-    if axes[chunks[-1][0]] == 0:
+        for done in ready_lines:
+            send_line(done)
+    if turned < count:
         turn(count - 1)
         send_line(count - 1)
     norm()
+    for which in range(t):
+        to_peer(sent[which], got[which], part_send.at[which], part_recv.at[0]).wait_send()
 
     for number in range(count):
         load(3, number).wait()
@@ -326,21 +364,23 @@
         line_n[pl.ds(j, 1), :] = whole_n[:, j * LANES : (j + 1) * LANES]
     compute_norm[...] = line_n[...].astype(jnp.bfloat16)
     for which in range(t):
-        to_peer(sent[which], got[which], part_send.at[which], part_recv.at[0]).wait_send()
         comp_half(which).wait()
     to_mate(line_got, line_got, line_recv.at[0], 0).wait_send()
 
 
 def drain(*refs):
     half = len(refs) // 2
-    sems = refs[-1]
-    copies = [
-        pltpu.make_async_copy(refs[i], refs[half + i], sems.at[i]) for i in range(half)
-    ]
-    for copy in copies:
-        copy.start()
-    for copy in copies:
-        copy.wait()
+
+    def run(sems):
+        copies = [
+            pltpu.make_async_copy(refs[i], refs[half + i], sems.at[i]) for i in range(half)
+        ]
+        for copy in copies:
+            copy.start()
+        for copy in copies:
+            copy.wait()
+
+    pl.run_scoped(run, pltpu.SemaphoreType.DMA((half,)))
 
 
 def exchange(m, args):
@@ -358,7 +398,6 @@
     count = sum(counts)
     share_n, width_n = master_norm.shape[0], partial_norm.shape[1]
     f32, bf16 = jnp.float32, jnp.bfloat16
-    dma = lambda *s: pltpu.SemaphoreType.DMA(s)
     out_shape = (
         [pltpu.VMEM(x.shape[1:], bf16) for x in partial]
         + [pltpu.VMEM((width_n // LANES, LANES), bf16)]
@@ -368,31 +407,21 @@
         [pltpu.VMEM(s, f32) for s in shapes]
         + [pltpu.VMEM(s, bf16) for s in pieces] * 2
         + [pltpu.VMEM(s, f32) for s in shapes]
-        + [pltpu.VMEM((1, share_n), f32)] * 4
         + [
+            pltpu.VMEM((3, 1, share_n), f32),
+            pltpu.VMEM((1, share_n), f32),
             pltpu.VMEM((1, width_n), f32),
             pltpu.VMEM((width_n // LANES, LANES), f32),
             pltpu.VMEM((count, 2, LANES), f32),
             pltpu.VMEM((count, m - 1, 2, LANES), f32),
             pltpu.VMEM((2, 2, LANES, LANES), f32),
             pltpu.VMEM((2, LANES, LANES), f32),
-            dma(count + 4),
-            dma(len(shapes)),
-            dma(count),
-            dma(len(shapes)),
-            dma(len(shapes)),
-            dma(1),
-            dma(count),
-            dma(3),
-            dma(2),
-            dma(2),
-            pltpu.SemaphoreType.REGULAR,
         ]
     )
     results = sum(math.prod(x.shape) * jnp.dtype(x.dtype).itemsize for x in out_shape)
     room = 63 * 2**20 - results
     outs = pl.pallas_call(
-        functools.partial(kernel, m, axes),
+        functools.partial(kernel, m, axes, count),
         out_shape=out_shape,
         in_specs=[pl.BlockSpec(memory_space=pltpu.HBM)] * 12,
         out_specs=[pl.BlockSpec(memory_space=pltpu.VMEM)] * 12,
@@ -408,7 +437,6 @@
         out_shape=[jax.ShapeDtypeStruct(x.shape, x.dtype) for x in outs],
         in_specs=[pl.BlockSpec(memory_space=pl.ANY)] * len(outs),
         out_specs=[pl.BlockSpec(memory_space=pltpu.HBM)] * len(outs),
-        scratch_shapes=[dma(len(outs))],
         compiler_params=pltpu.CompilerParams(vmem_limit_bytes=2**20),
     )(*outs)
     return [x.reshape(-1) if i % 4 == 3 else x for i, x in enumerate(outs)]

time: 19.6 us -> 18.5 us (0.944)
  Pallas kernels: 18.8 us -> 17.7 us
    pallas_call x1, Pallas kernels: 13.6 us -> 12.6 us  [exchange(): pl.pallas_call(functools.partial(kernel, m, axes, count), out_shape=out_s...]
where the time goes in v2:
time: 18.5 us; the launch traced here: 18.3 us
  Pallas kernels  17.7 us (96%)
  between operations  0.65 us (4%)
    pallas_call x1, Pallas kernels, exchange(): pl.pallas_call(functools.partial(kernel, m, axes, count), out_shape=out_s...  12.6 us
    pallas_call x1, Pallas kernels, exchange(): pl.pallas_call(drain, out_shape=[jax.ShapeDtypeStruct(x.shape, x.dtype) f...  5.07 us

profile of v2, /device:TPU:0, one launch (start us, length us, event | category | flops | bytes accessed | tf_op | source)
XLA Modules:
  0.0 18.3 jit_solution(9811549999854117351)
XLA Ops:
  0.6 12.6 %shard_map.211 = (bf16[1024,768]{1,0:T(8,128)(2,1)S(1)}, bf16[1024,768]{1,0:T(8,128)(2,1)S(1)}, bf16[768,1024]{1,0:T(8,128)(2,1)S(1)}, bf16[8,128]{1,0:T(8,128)(...) custom-call(f32[1,1024,768]{2,1,0:T(8,128)} %refs_0_.1, ...), custom_call_target="tpu_custom_call" | custom-call | tf_op jit(solution)/shard_map/pallas_call | solution.py:423
  13.2 5.1 %shard_map.212 = (bf16[1024,768]{1,0:T(8,128)(2,1)}, bf16[1024,768]{1,0:T(8,128)(2,1)}, bf16[768,1024]{1,0:T(8,128)(2,1)}, bf16[8,128]{1,0:T(8,128)(2,1)}, f32[5...) custom-call(bf16[1024,768]{1,0:T(8,128)(2,1)S(1)} %get-tuple-element, ...), custom_call_target="tpu_custom_call" | custom-call | tf_op jit(solution)/shard_map/pallas_call | solution.py:435

commit v3 on v2

--- a/solution.py
+++ b/solution.py
@@ -13,6 +13,7 @@
 MESH = pl.DeviceIdType.MESH
 LANES = 128
 CODE_SCALE = 2.0**13
+EXTRA = 2
 
 
 def cut(ref, axis, start, size):
@@ -45,11 +46,16 @@
         sems(2),
         sems(2),
         pltpu.SemaphoreType.REGULAR,
+        sems(EXTRA),
+        sems(EXTRA),
+        sems(1),
+        sems(EXTRA),
     )
 
 
 def body(m, axes, refs, load_sem, part_send, part_recv, comp_recv, *more):
-    line_send, line_recv, norm_load_sem, norm_send, norm_recv, ready = more
+    line_send, line_recv, norm_load_sem, norm_send, norm_recv, ready = more[:6]
+    extra_send, extra_recv, cross_send, cross_recv = more[6:]
     refs = list(refs)
     take = lambda count: [refs.pop(0) for _ in range(count)]
     t = len(axes)
@@ -62,7 +68,7 @@
     other, sent, got, memory = take(t), take(t), take(t), take(t)
     master, mean = stepped, state
     own_norm, got_n, whole_n, line_n = take(4)
-    line, line_got, fold, tile = take(4)
+    line, line_got, fold, tile, extra, extra_got, cross = take(7)
 
     me = lax.axis_index("replica")
     at = lax.axis_index("model")
@@ -81,7 +87,7 @@
     def slot_of(kind, number):
         if kind == 0:
             return count + number if number < lead else number + 1 - lead
-        return number
+        return 2 * count - 1 - number if kind == 3 and number >= count - EXTRA else number
 
     def load(kind, number):
         which, c = chunks[number]
@@ -138,7 +144,8 @@
     def comp_half(which):
         axis = axes[which]
         share = mean[which].shape[axis]
-        mine = cut(compute[which], axis, pl.multiple_of(me * share, LANES), share)
+        size = share - EXTRA * LANES * (which == t - 1)
+        mine = cut(compute[which], axis, pl.multiple_of(me * share, LANES), size)
         return to_peer(mine, mine, part_send.at[which], comp_recv.at[which])
 
     peer_n = pl.ds(pl.multiple_of(peer * share_n, LANES), share_n)
@@ -159,6 +166,23 @@
 
     def line_copy(number, k):
         return to_mate(line.at[number], line_got.at[number, k], line_recv.at[number], k)
+
+    first = count - EXTRA
+
+    def extra_copy(number):
+        x = number - first
+        return to_peer(extra.at[x], extra_got.at[x], extra_send.at[x], extra_recv.at[x])
+
+    def cross_copy(number, k):
+        where = {"replica": peer} if k == 0 else {"model": mates[k - 1], "replica": peer}
+        return pltpu.make_async_remote_copy(
+            src_ref=line.at[number],
+            dst_ref=cross.at[number - first, k],
+            send_sem=cross_send.at[0],
+            recv_sem=cross_recv.at[number - first],
+            device_id=where,
+            device_id_type=MESH,
+        )
 
     def blocks(number):
         which, c = chunks[number]
@@ -216,6 +240,9 @@
     def send_line(number):
         for k in range(m - 1):
             line_copy(number, k).start()
+        if number >= first:
+            for k in range(m):
+                cross_copy(number, k).start()
 
     def ratio_of(number):
         both = line[number]
@@ -252,6 +279,26 @@
             new = master[which][block] - learn_rate * new
             stepped[which][block] = new
             compute[which][target] = new.astype(jnp.bfloat16)
+
+    def pack(number):
+        which, c = chunks[number]
+        for inside, block in blocks(number):
+            extra[(number - first, 0, *inside)] = code(mean[which][block])
+            rest = master[which][block] - learn_rate * hold_rate * memory[which][block]
+            extra[(number - first, 1, *inside)] = code(rest)
+
+    def finish(number):
+        which, c = chunks[number]
+        x = number - first
+        share = mean[which].shape[axes[which]]
+        both = sum(cross[x, k] for k in range(m))
+        scale = learn_rate * rate * jnp.sqrt(both[0:1])
+        scale = scale * lax.rsqrt(both[1:2] * rate**2 + 1e-06)
+        base = pl.multiple_of(peer * share + c * LANES, LANES)
+        for inside, block in blocks(number):
+            total = decode(extra_got[(x, 0, *inside)])
+            rest = decode(extra_got[(x, 1, *inside)])
+            compute[which][inside[0], pl.ds(base, LANES)] = (rest - total * scale).astype(jnp.bfloat16)
 
     def norm():
         pltpu.make_async_copy(own_norm, own_norm, norm_load_sem.at[0]).wait()
@@ -330,7 +377,7 @@
             part_copy(number + lead - 1).start()
         for later in range(2 * (number - 6), 2 * (number - 5)):
             if 0 <= later < count:
-                load(3, later).start()
+                load(3, (later - EXTRA) % count).start()
         if number == 0:
 
             @pl.when(me == 0)
@@ -351,14 +398,26 @@
     for which in range(t):
         to_peer(sent[which], got[which], part_send.at[which], part_recv.at[0]).wait_send()
 
+    for number in range(first, count):
+        load(3, number).wait()
+        pack(number)
+        extra_copy(number).start()
     for number in range(count):
-        load(3, number).wait()
+        if number < first:
+            load(3, number).wait()
         wait_line(number)
         if axes[chunks[number][0]] == 0:
             spread(number)
         update(number)
-        comp_copy(number).start()
-
+        if number < first:
+            comp_copy(number).start()
+
+    for number in range(first, count):
+        extra_copy(number).wait()
+        arrived = cross.at[number - first]
+        to_peer(arrived, arrived, cross_send.at[0], cross_recv.at[number - first]).wait_recv()
+        finish(number)
+    to_peer(cross, cross, cross_send.at[0], cross_recv.at[0]).wait_send()
     whole_norm_copy.wait()
     for j in range(whole_n.shape[1] // LANES):
         line_n[pl.ds(j, 1), :] = whole_n[:, j * LANES : (j + 1) * LANES]
@@ -416,6 +475,9 @@
             pltpu.VMEM((count, m - 1, 2, LANES), f32),
             pltpu.VMEM((2, 2, LANES, LANES), f32),
             pltpu.VMEM((2, LANES, LANES), f32),
+            pltpu.VMEM((EXTRA, 2, shapes[-1][0], LANES), bf16),
+            pltpu.VMEM((EXTRA, 2, shapes[-1][0], LANES), bf16),
+            pltpu.VMEM((EXTRA, m, 2, LANES), f32),
         ]
     )
     results = sum(math.prod(x.shape) * jnp.dtype(x.dtype).itemsize for x in out_shape)

time: 18.5 us -> 17.9 us (0.968)
  Pallas kernels: 17.7 us -> 17.1 us
    pallas_call x1, Pallas kernels: 12.6 us -> 12 us  [exchange(): pl.pallas_call(functools.partial(kernel, m, axes, count), out_shape=out_s...]
where the time goes in v3:
time: 17.9 us; the launch traced here: 17.8 us
  Pallas kernels  17.1 us (96%)
  between operations  0.65 us (4%)
    pallas_call x1, Pallas kernels, exchange(): pl.pallas_call(functools.partial(kernel, m, axes, count), out_shape=out_s...  12 us
    pallas_call x1, Pallas kernels, exchange(): pl.pallas_call(drain, out_shape=[jax.ShapeDtypeStruct(x.shape, x.dtype) f...  5.07 us

profile of v3, /device:TPU:0, one launch (start us, length us, event | category | flops | bytes accessed | tf_op | source)
XLA Modules:
  0.0 17.8 jit_solution(11048185171190019386)
XLA Ops:
  0.6 12.0 %shard_map.211 = (bf16[1024,768]{1,0:T(8,128)(2,1)S(1)}, bf16[1024,768]{1,0:T(8,128)(2,1)S(1)}, bf16[768,1024]{1,0:T(8,128)(2,1)S(1)}, bf16[8,128]{1,0:T(8,128)(...) custom-call(f32[1,1024,768]{2,1,0:T(8,128)} %refs_0_.1, ...), custom_call_target="tpu_custom_call" | custom-call | tf_op jit(solution)/shard_map/pallas_call | solution.py:485
  12.7 5.1 %shard_map.212 = (bf16[1024,768]{1,0:T(8,128)(2,1)}, bf16[1024,768]{1,0:T(8,128)(2,1)}, bf16[768,1024]{1,0:T(8,128)(2,1)}, bf16[8,128]{1,0:T(8,128)(2,1)}, f32[5...) custom-call(bf16[1024,768]{1,0:T(8,128)(2,1)S(1)} %get-tuple-element, ...), custom_call_target="tpu_custom_call" | custom-call | tf_op jit(solution)/shard_map/pallas_call | solution.py:497

commit v4 on v3

--- a/solution.py
+++ b/solution.py
@@ -82,7 +82,7 @@
         chunks += [(which, c) for c in range(share // LANES)]
     for c in range(2):
         chunks.insert(c, chunks.pop(chunks.index((t - 1, c))))
-    count, lead = len(chunks), 8
+    count, lead = len(chunks), 6
 
     def slot_of(kind, number):
         if kind == 0:

time: 17.9 us -> 18.3 us (1.022)
  Pallas kernels: 17.1 us -> 17.5 us
    pallas_call x1, Pallas kernels: 12 us -> 12.4 us  [exchange(): pl.pallas_call(functools.partial(kernel, m, axes, count), out_shape=out_s...]
where the time goes in v4:
time: 18.3 us; the launch traced here: 18.2 us
  Pallas kernels  17.5 us (96%)
  between operations  0.65 us (4%)
    pallas_call x1, Pallas kernels, exchange(): pl.pallas_call(functools.partial(kernel, m, axes, count), out_shape=out_s...  12.4 us
    pallas_call x1, Pallas kernels, exchange(): pl.pallas_call(drain, out_shape=[jax.ShapeDtypeStruct(x.shape, x.dtype) f...  5.07 us

profile of v4, /device:TPU:0, one launch (start us, length us, event | category | flops | bytes accessed | tf_op | source)
XLA Modules:
  0.0 18.2 jit_solution(12245553887315835789)
XLA Ops:
  0.6 12.4 %shard_map.211 = (bf16[1024,768]{1,0:T(8,128)(2,1)S(1)}, bf16[1024,768]{1,0:T(8,128)(2,1)S(1)}, bf16[768,1024]{1,0:T(8,128)(2,1)S(1)}, bf16[8,128]{1,0:T(8,128)(...) custom-call(f32[1,1024,768]{2,1,0:T(8,128)} %refs_0_.1, ...), custom_call_target="tpu_custom_call" | custom-call | tf_op jit(solution)/shard_map/pallas_call | solution.py:485
  13.1 5.1 %shard_map.212 = (bf16[1024,768]{1,0:T(8,128)(2,1)}, bf16[1024,768]{1,0:T(8,128)(2,1)}, bf16[768,1024]{1,0:T(8,128)(2,1)}, bf16[8,128]{1,0:T(8,128)(2,1)}, f32[5...) custom-call(bf16[1024,768]{1,0:T(8,128)(2,1)S(1)} %get-tuple-element, ...), custom_call_target="tpu_custom_call" | custom-call | tf_op jit(solution)/shard_map/pallas_call | solution.py:497
